TPU v7x, 128 devices: a whole 4x4x4 slice. The times are simulated.
128 devices in a mesh: ctx: 16 (over x, z), tp: 8 (over y, core).
Axes of the slice: x: 4, y: 4, z: 4, core: 2. Of those that a mesh axis runs over, the one named last changes fastest.
Arguments:
- queries: bfloat16 [512, 8192], P('ctx', 'tp'), may hold values from -6 to 6
- cache_keys: bfloat16 [65536, 1024], P('ctx', 'tp'), may hold values from -18 to 18
- cache_values: bfloat16 [65536, 1024], P('ctx', 'tp'), may hold values from -6 to 6
- span_keys: bfloat16 [512, 1024], P('ctx', 'tp'), may hold values from -24 to 24
- span_values: bfloat16 [512, 1024], P('ctx', 'tp'), may hold values from -6 to 6
- out_weight: bfloat16 [8192, 8192], P('tp', 'ctx'), may hold values from -0.0625 to 0.0625
- residual: bfloat16 [512, 8192], P('tp', 'ctx'), may hold values from -72 to 72
- norm_gain: bfloat16 [8192], P('ctx'), may hold values from 0.5 to 1.5
- head_weight: bfloat16 [8192, 128256], P(None, ('ctx', 'tp')), may hold values from -0.198873782 to 0.198873782
- targets: int32 [512], replicated, may hold values from 0 to 128255
- window_lengths: int32 [8], replicated, may hold values from 1 to 128, 512 in all
Outputs:
- token_logprob: float32 [512], P('ctx')
- window_means: float32 [8], replicated
Inputs may be any that keep to these rules, and one draw needn't show every extreme that they name: `window_lengths`: the 8 lengths sum to 512.
All inputs are finite; a program needn't handle non-finite values.
Results may differ from a plain program's by a relative error of at most 0.0025.
Values may be sent and summed in bfloat16 or wider, within the bound.
No kernel may reach another device: no remote copies, remote signals or barrier semaphores. Data moves between devices by JAX's collectives and lax.ppermute only.
A program may use at most 128 MiB of HBM per device.

v0:
```python
import jax
import jax.numpy as jnp
from jax import lax
from jax.sharding import Mesh
from jax.sharding import PartitionSpec as P

D = 8192
HEADS = 64
KV_HEADS = 8
HD = 128
CTX = ("ctx_0", "ctx_1")
TP = ("tp_0", "tp_1")
CTX_TP = ("ctx_0", "ctx_1", "tp_0", "tp_1")
EPSILON = 1e-05
NEGATIVE = -1e30


def in_order(blocks, dim):
    blocks = jnp.moveaxis(blocks, 0, dim)
    shape = blocks.shape
    return blocks.reshape(*shape[:dim], shape[dim] * shape[dim + 1], *shape[dim + 2 :])


def sent_to_all(value, axis):
    count = lax.axis_size(axis)
    return lax.all_to_all(
        jnp.broadcast_to(value[None], (count, *value.shape)), axis, 0, 0, tiled=True
    )


def gathered_copies(value, axis, dim):
    return in_order(sent_to_all(value, axis), dim)


def sent_together(arrays, axis, split_dim, concat_dim, along):
    ends, at = ([], 0)
    for a in arrays[:-1]:
        at += a.shape[along]
        ends.append(at)
    both = jnp.concatenate(arrays, axis=along)
    return tuple(
        jnp.split(
            lax.all_to_all(both, axis, split_axis=split_dim, concat_axis=concat_dim, tiled=True),
            ends,
            axis=along,
        )
    )


def in_blocks(value, dim, count):
    shape = value.shape
    blocks = value.reshape(*shape[:dim], count, shape[dim] // count, *shape[dim + 1 :])
    return jnp.moveaxis(blocks, dim, 0)


def summed_on_arrival(value, axis, dim):
    blocks = in_blocks(value, dim, lax.axis_size(axis))
    arrived = lax.all_to_all(blocks, axis, split_axis=0, concat_axis=0, tiled=True)
    return arrived.astype(jnp.float32).sum(axis=0)


def over_axes(value, axes):
    for axis in axes:
        value = lax.psum(value, axis)
    return value


def gathered_once(value, axis):
    leaves = jax.tree.leaves(value)
    order = sorted(range(len(leaves)), key=lambda k: -leaves[k].size)
    width = (1, *leaves[order[0]].shape)[-1]
    lines = [
        jnp.pad(leaves[k].reshape(-1), (0, -leaves[k].size % width)).reshape(-1, width)
        for k in order
    ]
    both, at, found = (lax.all_gather(jnp.concatenate(lines), axis), 0, {})
    for k, line in zip(order, lines):
        slab = both[:, at : at + len(line)].reshape(len(both), -1)
        found[k] = slab[:, : leaves[k].size].reshape(-1, *leaves[k].shape)
        at += len(line)
    numbers = iter(range(len(leaves)))
    return jax.tree.map(lambda _: found[next(numbers)], value)


def combined_by_axis(value, axes, combine):
    for axis in axes:
        pieces = gathered_once(value, axis)
        value = jax.tree.map(lambda part: part[0], pieces)
        for k in range(1, lax.axis_size(axis)):
            value = combine(value, jax.tree.map(lambda part: part[k], pieces))
    return value


def fold_block(state, scores, value_rows):
    row_max, row_sum, weighted = state
    new_max = jnp.maximum(row_max, jnp.max(scores, axis=1))
    fading = jnp.exp(row_max - new_max)
    weights = jnp.exp(scores - new_max[:, None])
    row_sum = row_sum * fading + jnp.sum(weights, axis=1)
    weighted = weighted * fading[:, None] + jnp.dot(
        weights.astype(jnp.bfloat16), value_rows, preferred_element_type=jnp.float32
    )
    return (new_max, row_sum, weighted)


def partial_head(
    query_rows, cache_part, value_part, fresh_keys, fresh_values, first_token, span_total
):
    row_count = query_rows.shape[0]
    scaling = HD ** (-0.5)
    block_size = min(1024, cache_part.shape[0])
    block_count = cache_part.shape[0] // block_size
    key_blocks = cache_part.reshape(block_count, block_size, HD)
    value_blocks = value_part.reshape(block_count, block_size, HD)

    def advance(state, block_pair):
        scores = jnp.dot(query_rows, block_pair[0].T, preferred_element_type=jnp.float32) * scaling
        return (fold_block(state, scores, block_pair[1]), None)

    start_state = (
        jnp.full((row_count,), NEGATIVE, jnp.float32),
        jnp.zeros((row_count,), jnp.float32),
        jnp.zeros((row_count, HD), jnp.float32),
    )
    state, unused = lax.scan(advance, start_state, (key_blocks, value_blocks))
    scores = jnp.dot(query_rows, fresh_keys.T, preferred_element_type=jnp.float32) * scaling
    token_of_row = jnp.arange(row_count, dtype=jnp.int32) % span_total
    key_token = first_token + jnp.arange(fresh_keys.shape[0], dtype=jnp.int32)
    scores = jnp.where(token_of_row[:, None] >= key_token[None, :], scores, NEGATIVE)
    return fold_block(state, scores, fresh_values)


def combine_logits(first, second):
    row_max = jnp.maximum(first[0], second[0])
    row_sum = first[1] * jnp.exp(first[0] - row_max) + second[1] * jnp.exp(second[0] - row_max)
    return (row_max, row_sum, first[2] + second[2])


def local(
    queries,
    cache_keys,
    cache_values,
    span_keys,
    span_values,
    out_weight,
    residual,
    norm_gain,
    head_weight,
    targets,
    window_lengths,
):
    ctx_rank = lax.axis_index(CTX)
    span_dev = queries.shape[0]
    group_size = HEADS // KV_HEADS
    kv_local = cache_keys.shape[1] // HD
    heads_local = kv_local * group_size
    query_all = gathered_copies(queries, CTX, 0)
    span_total = query_all.shape[0]
    query_heads = (
        query_all.reshape(span_total, kv_local, group_size, HD)
        .transpose(1, 2, 0, 3)
        .reshape(kv_local, group_size * span_total, HD)
    )
    first_token = ctx_rank * span_dev
    row_max, row_sum, weighted = partial_head(
        query_heads[0], cache_keys, cache_values, span_keys, span_values, first_token, span_total
    )
    maxima = [row_max]
    totals = [row_sum]
    weighted_rows = [weighted]
    part_max = (
        jnp.stack(maxima)
        .reshape(kv_local, group_size, span_total)
        .transpose(2, 0, 1)
        .reshape(span_total, heads_local)
    )
    part_sum = (
        jnp.stack(totals)
        .reshape(kv_local, group_size, span_total)
        .transpose(2, 0, 1)
        .reshape(span_total, heads_local)
    )
    part_weighted = (
        jnp.stack(weighted_rows)
        .reshape(kv_local, group_size, span_total, HD)
        .transpose(2, 0, 1, 3)
        .reshape(span_total, heads_local * HD)
    )
    pieces = tuple(
        (
            part.astype(jnp.float32)
            for part in sent_together(
                (
                    part_max[None].astype(jnp.bfloat16),
                    part_sum[None].astype(jnp.bfloat16),
                    part_weighted[None].astype(jnp.bfloat16),
                ),
                CTX,
                1,
                0,
                2,
            )
        )
    )
    source_count = pieces[0].shape[0]
    row_max = jnp.max(pieces[0], axis=0)
    fading = jnp.exp(pieces[0] - row_max[None])
    row_sum = jnp.sum(pieces[1] * fading, axis=0)
    weighted = jnp.sum(
        pieces[2].reshape(source_count, span_dev, heads_local, HD) * fading[:, :, :, None], axis=0
    )
    attended_own = (
        (weighted / row_sum[:, :, None]).reshape(span_dev, heads_local * HD).astype(jnp.bfloat16)
    )
    attended_all = gathered_copies(attended_own, CTX, 0)
    projected = summed_on_arrival(
        jnp.dot(attended_all, out_weight, preferred_element_type=jnp.float32).astype(jnp.bfloat16),
        TP,
        0,
    )
    stream = residual.astype(jnp.float32) + projected
    squares = over_axes(jnp.sum(stream * stream, axis=1), CTX)
    scaled = lax.rsqrt(squares / D + EPSILON)
    normed_part = (stream * scaled[:, None] * norm_gain.astype(jnp.float32)[None, :]).astype(
        jnp.bfloat16
    )
    normed_rows = gathered_copies(normed_part, CTX, 1)
    logits = jnp.dot(
        lax.all_gather(normed_rows, TP, axis=0, tiled=True),
        head_weight,
        preferred_element_type=jnp.float32,
    )
    vocab_dev = head_weight.shape[1]
    vocab_start = lax.axis_index(CTX_TP) * vocab_dev
    columns = vocab_start + jnp.arange(vocab_dev, dtype=jnp.int32)
    target_part = jnp.sum(jnp.where(targets[:, None] == columns[None, :], logits, 0.0), axis=1)
    local_max = jnp.max(logits, axis=1)
    exp_part = jnp.sum(jnp.exp(logits - local_max[:, None]), axis=1)
    global_max, exp_total, target_logit = combined_by_axis(
        (local_max, exp_part, target_part), CTX_TP, combine_logits
    )
    token_logprob = target_logit - (global_max + jnp.log(exp_total))
    window_ends = jnp.cumsum(window_lengths)
    window_starts = window_ends - window_lengths
    positions = jnp.arange(span_total, dtype=jnp.int32)
    member = (
        (positions[None, :] >= window_starts[:, None]) & (positions[None, :] < window_ends[:, None])
    ).astype(jnp.float32)
    window_sums = jnp.dot(member, token_logprob)
    window_means = window_sums / window_lengths.astype(jnp.float32)
    own_logprob = lax.dynamic_slice_in_dim(token_logprob, first_token, span_dev, 0)
    return (own_logprob, window_means)


def solution(mesh):
    split = Mesh(mesh.devices.reshape(4, 4, 4, 2), ("ctx_0", "ctx_1", "tp_0", "tp_1"))
    in_specs = (
        P(CTX, TP),
        P(CTX, TP),
        P(CTX, TP),
        P(CTX, TP),
        P(CTX, TP),
        P(TP, CTX),
        P(TP, CTX),
        P(CTX),
        P(None, CTX_TP),
        P(),
        P(),
    )
    out_specs = (P(CTX), P())
    return jax.shard_map(local, mesh=split, in_specs=in_specs, out_specs=out_specs, check_vma=False)
```

profile of v0, /device:TPU:1, one launch (start us, length us, event | category | flops | bytes accessed | tf_op | source)
XLA Modules:
  0.0 373.4 jit_solution(12038084039484746735)
XLA Ops:
  7.2 0.0 copy-start
  7.2 2.1 broadcast_in_dim.24
  9.3 8.5 %all-to-all-start = ((bf16[16,32,1024]{2,1,0:T(8,128)(2,1)}), bf16[16,32,1024]{2,1,0:T(8,128)(2,1)}, u32[]{:S(2)}, u32[]{:S(2)}) async-start(bf16[16,32,1024]{2,1,0:T(8,128)(2,1)} %broadcast_in_dim.24), calls=%async_computation | async-start | bytes 2097152 | tf_op jit(solution)/shard_map/all_to_all | solution.py:26
  17.8 15.7 %all-to-all-done = bf16[16,32,1024]{2,1,0:T(8,128)(2,1)} async-done(((bf16[16,32,1024]{2,1,0:T(8,128)(2,1)}), bf16[16,32,1024]{2,1,0:T(8,128)(2,1)}, u32[]{:S(2)}, u32[]{:S(2)}) %all-to-all-start) | async-done | bytes 1048608 | tf_op jit(solution)/shard_map/all_to_all | solution.py:26
  33.5 1.5 copy.25
  35.0 1.2 copy.19
  36.1 102.5 %while.15 = (s32[]{:T(128)}, f32[4096]{0:T(1024)S(1)}, f32[4096]{0:T(1024)S(1)}, f32[4096,128]{1,0:T(8,128)S(1)}, bf16[4,1024,128]{2,1,0:T(8,128)(2,1)}, /*index...) while((s32[]{:T(128)}, f32[4096]{0:T(1024)S(1)}, ...), condition=%wide.region_3.4_spmd.clone, body=%wide.region_0.3_spmd.clone.sunk | while | flops 2182631424 | bytes 56361076 | solution.py:125
  36.1 9.4 %multiply_reduce_fusion.5 = (f32[4096]{0:T(1024)S(1)}, f32[1024,4096]{1,0:T(8,128)}) fusion(bf16[4096,128]{1,0:T(8,128)(2,1)} %get-tuple-element.183, bf16[4,1024,128]{2,1,0:T(8,128)(2,1)} %get-tuple-element.182, s32[]{:T(128)S(6)} %copy.32), kind=kOutput, calls=%fused_computation.1.clone.1 | convolution fusion | flops 1082126336 | bytes 18104324 | tf_op jit(solution)/shard_map/while/body/eval_jaxpr/dot_general | solution.py:117
  45.5 8.5 %fusion.99 = f32[4096]{0:T(1024)S(1)} fusion(f32[1024,4096]{1,0:T(8,128)} %get-tuple-element.157, f32[4096]{0:T(1024)S(1)} %select_maximum_fusion.2), kind=kLoop, calls=%fused_computation.3.clone.1 | loop fusion | flops 12578816 | bytes 16809984 | tf_op jit(solution)/shard_map/while/body/eval_jaxpr/reduce_sum | solution.py:99
  54.1 7.7 %fusion.101 = f32[4096,128]{1,0:T(8,128)S(1)} fusion(f32[1024,4096]{1,0:T(8,128)} %get-tuple-element.157, f32[4096]{0:T(1024)S(1)} %select_maximum_fusion.2, f32[4096,128]{1,0:T(8,128)S(1)} %get-tuple-element.172, f32[4096]{0:T(1024)S(1)} %get-tuple-element.159, pred[]{:T(512)S(6)} %compare.4, bf16[4,1024,128]{2,1,0:T(8,128)(2,1)} %get-tuple-element.184, ...), kind=kOutput, calls=%fused_computation.7.clone.1 | convolution fusion | flops 1087897600 | bytes 21266436 | tf_op jit(solution)/shard_map/while/body/eval_jaxpr/dot_general | solution.py:100
  61.8 9.4 %multiply_reduce_fusion.5 = (f32[4096]{0:T(1024)S(1)}, f32[1024,4096]{1,0:T(8,128)}) fusion(bf16[4096,128]{1,0:T(8,128)(2,1)} %get-tuple-element.183, bf16[4,1024,128]{2,1,0:T(8,128)(2,1)} %get-tuple-element.182, s32[]{:T(128)S(6)} %copy.32), kind=kOutput, calls=%fused_computation.1.clone.1 | convolution fusion | flops 1082126336 | bytes 18104324 | tf_op jit(solution)/shard_map/while/body/eval_jaxpr/dot_general | solution.py:117
  71.1 8.5 %fusion.99 = f32[4096]{0:T(1024)S(1)} fusion(f32[1024,4096]{1,0:T(8,128)} %get-tuple-element.157, f32[4096]{0:T(1024)S(1)} %select_maximum_fusion.2), kind=kLoop, calls=%fused_computation.3.clone.1 | loop fusion | flops 12578816 | bytes 16809984 | tf_op jit(solution)/shard_map/while/body/eval_jaxpr/reduce_sum | solution.py:99
  79.7 7.7 %fusion.101 = f32[4096,128]{1,0:T(8,128)S(1)} fusion(f32[1024,4096]{1,0:T(8,128)} %get-tuple-element.157, f32[4096]{0:T(1024)S(1)} %select_maximum_fusion.2, f32[4096,128]{1,0:T(8,128)S(1)} %get-tuple-element.172, f32[4096]{0:T(1024)S(1)} %get-tuple-element.159, pred[]{:T(512)S(6)} %compare.4, bf16[4,1024,128]{2,1,0:T(8,128)(2,1)} %get-tuple-element.184, ...), kind=kOutput, calls=%fused_computation.7.clone.1 | convolution fusion | flops 1087897600 | bytes 21266436 | tf_op jit(solution)/shard_map/while/body/eval_jaxpr/dot_general | solution.py:100
  87.4 9.4 %multiply_reduce_fusion.5 = (f32[4096]{0:T(1024)S(1)}, f32[1024,4096]{1,0:T(8,128)}) fusion(bf16[4096,128]{1,0:T(8,128)(2,1)} %get-tuple-element.183, bf16[4,1024,128]{2,1,0:T(8,128)(2,1)} %get-tuple-element.182, s32[]{:T(128)S(6)} %copy.32), kind=kOutput, calls=%fused_computation.1.clone.1 | convolution fusion | flops 1082126336 | bytes 18104324 | tf_op jit(solution)/shard_map/while/body/eval_jaxpr/dot_general | solution.py:117
  96.8 8.5 %fusion.99 = f32[4096]{0:T(1024)S(1)} fusion(f32[1024,4096]{1,0:T(8,128)} %get-tuple-element.157, f32[4096]{0:T(1024)S(1)} %select_maximum_fusion.2), kind=kLoop, calls=%fused_computation.3.clone.1 | loop fusion | flops 12578816 | bytes 16809984 | tf_op jit(solution)/shard_map/while/body/eval_jaxpr/reduce_sum | solution.py:99
  105.3 7.7 %fusion.101 = f32[4096,128]{1,0:T(8,128)S(1)} fusion(f32[1024,4096]{1,0:T(8,128)} %get-tuple-element.157, f32[4096]{0:T(1024)S(1)} %select_maximum_fusion.2, f32[4096,128]{1,0:T(8,128)S(1)} %get-tuple-element.172, f32[4096]{0:T(1024)S(1)} %get-tuple-element.159, pred[]{:T(512)S(6)} %compare.4, bf16[4,1024,128]{2,1,0:T(8,128)(2,1)} %get-tuple-element.184, ...), kind=kOutput, calls=%fused_computation.7.clone.1 | convolution fusion | flops 1087897600 | bytes 21266436 | tf_op jit(solution)/shard_map/while/body/eval_jaxpr/dot_general | solution.py:100
  113.0 9.4 %multiply_reduce_fusion.5 = (f32[4096]{0:T(1024)S(1)}, f32[1024,4096]{1,0:T(8,128)}) fusion(bf16[4096,128]{1,0:T(8,128)(2,1)} %get-tuple-element.183, bf16[4,1024,128]{2,1,0:T(8,128)(2,1)} %get-tuple-element.182, s32[]{:T(128)S(6)} %copy.32), kind=kOutput, calls=%fused_computation.1.clone.1 | convolution fusion | flops 1082126336 | bytes 18104324 | tf_op jit(solution)/shard_map/while/body/eval_jaxpr/dot_general | solution.py:117
  122.4 8.5 %fusion.99 = f32[4096]{0:T(1024)S(1)} fusion(f32[1024,4096]{1,0:T(8,128)} %get-tuple-element.157, f32[4096]{0:T(1024)S(1)} %select_maximum_fusion.2), kind=kLoop, calls=%fused_computation.3.clone.1 | loop fusion | flops 12578816 | bytes 16809984 | tf_op jit(solution)/shard_map/while/body/eval_jaxpr/reduce_sum | solution.py:99
  131.0 7.7 %fusion.101 = f32[4096,128]{1,0:T(8,128)S(1)} fusion(f32[1024,4096]{1,0:T(8,128)} %get-tuple-element.157, f32[4096]{0:T(1024)S(1)} %select_maximum_fusion.2, f32[4096,128]{1,0:T(8,128)S(1)} %get-tuple-element.172, f32[4096]{0:T(1024)S(1)} %get-tuple-element.159, pred[]{:T(512)S(6)} %compare.4, bf16[4,1024,128]{2,1,0:T(8,128)(2,1)} %get-tuple-element.184, ...), kind=kOutput, calls=%fused_computation.7.clone.1 | convolution fusion | flops 1087897600 | bytes 21266436 | tf_op jit(solution)/shard_map/while/body/eval_jaxpr/dot_general | solution.py:100
  138.7 0.0 copy-start.4
  138.7 1.7 fusion.79
  140.4 0.1 fusion.22
  140.5 1.8 fusion.18
  142.4 1.5 copy.20
  143.9 1.1 pad_maximum_fusion
  145.0 5.2 %copy.21 = bf16[1,512,1040]{2,0,1:T(2,128)(2,1)S(1)} copy(bf16[1,512,1040]{1,2,0:T(8,128)(2,1)} %pad_maximum_fusion) | data formatting | bytes 2129920 | tf_op jit(solution)/shard_map/concatenate | solution.py:40
  150.2 0.5 broadcast.82
  150.8 9.2 %reduce.4 = bf16[512,1040]{1,0:T(8,128)(2,1)} reduce(bf16[512,1,1040]{2,1,0:T(2,128)(2,1)S(1)} %bitcast.306, bf16[]{:T(256)} %broadcast.82), dimensions={1}, to_apply=%bitcast.273.reduce_sub_computation | reduce | bytes 2129922
  159.9 3.9 %reshape.901 = bf16[16,2,16640]{2,1,0:T(2,128)(2,1)S(1)} reshape(bf16[512,1040]{1,0:T(8,128)(2,1)} %reduce.4) | data formatting | bytes 2129920
  163.8 18.9 %all_to_all.32 = bf16[16,2,16640]{2,1,0:T(2,128)(2,1)} all-to-all(bf16[16,2,16640]{2,1,0:T(2,128)(2,1)S(1)} %reshape.901), channel_id=1, replica_groups=mesh['ctx_0'=4,'ctx_1'=4,'tp_0'=4,'tp_1'=2] {'ctx_0','ctx_1'}, dimensions={0} | all-to-all | bytes 2129920 | tf_op jit(solution)/shard_map/all_to_all | solution.py:43
  182.7 4.8 %reshape.902 = bf16[512,1,1040]{2,1,0:T(2,128)(2,1)S(1)} reshape(bf16[16,2,16640]{2,1,0:T(2,128)(2,1)} %all_to_all.32) | data formatting | bytes 2129920
  187.6 0.2 copy.23
  187.8 0.1 multiply_reduce_fusion.2
  187.9 0.9 copy-done.1
  188.8 2.0 mul.276
  190.7 1.7 mul.277
  192.4 1.8 multiply_reduce_fusion.1
  194.2 0.1 div.24
  194.4 0.1 broadcast_in_dim.26
  194.5 16.1 %all_to_all.33 = bf16[16,32,1024]{2,1,0:T(8,128)(2,1)S(1)} all-to-all(bf16[16,32,1024]{2,1,0:T(8,128)(2,1)S(1)} %broadcast_in_dim.26), channel_id=1, replica_groups=mesh['ctx_0'=4,'ctx_1'=4,'tp_0'=4,'tp_1'=2] {'ctx_0','ctx_1'}, dimensions={0} | all-to-all | bytes 2097152 | tf_op jit(solution)/shard_map/all_to_all | solution.py:26
  210.6 1.5 convolution_convert_fusion
  212.1 9.2 %all-to-all-start.3 = ((bf16[8,64,512]{2,1,0:T(8,128)(2,1)}), bf16[8,64,512]{2,1,0:T(8,128)(2,1)S(1)}, u32[]{:S(2)}, u32[]{:S(2)}) async-start(bf16[8,64,512]{2,1,0:T(8,128)(2,1)} %bitcast.12), calls=%async_computation.3 | async-start | bytes 1048576 | tf_op jit(solution)/shard_map/all_to_all | solution.py:58
  221.3 0.0 all-gather.10.cloned.1.call-start
  221.3 9.3 %all-to-all-done.3 = bf16[8,64,512]{2,1,0:T(8,128)(2,1)S(1)} async-done(((bf16[8,64,512]{2,1,0:T(8,128)(2,1)}), bf16[8,64,512]{2,1,0:T(8,128)(2,1)S(1)}, u32[]{:S(2)}, u32[]{:S(2)}) %all-to-all-start.3) | async-done | bytes 524320 | tf_op jit(solution)/shard_map/all_to_all | solution.py:58
  230.6 0.1 convert_reduce_fusion
  230.7 0.0 copy-done.2
  230.7 0.1 multiply_reduce_fusion.3
  230.8 6.8 %psum.14 = f32[64]{0:T(128)S(1)} all-reduce(f32[64]{0:T(128)S(1)} %multiply_reduce_fusion.3), channel_id=1, replica_groups=mesh['ctx_0'=4,'ctx_1'=4,'tp_0'=4,'tp_1'=2] {'ctx_0'}, use_global_device_ids=true, to_apply=%region_11.12 | all-reduce | flops 64 | bytes 512 | tf_op jit(solution)/shard_map/psum | solution.py:64
  237.7 6.3 %psum.15 = f32[64]{0:T(128)S(1)} all-reduce(f32[64]{0:T(128)S(1)} %psum.14), channel_id=1, replica_groups=mesh['ctx_0'=4,'ctx_1'=4,'tp_0'=4,'tp_1'=2] {'ctx_1'}, use_global_device_ids=true, to_apply=%region_12.13 | all-reduce | flops 64 | bytes 512 | tf_op jit(solution)/shard_map/psum | solution.py:64
  244.0 0.1 multiply_convert_fusion
  244.1 0.1 broadcast_in_dim.27
  244.2 15.1 %all_to_all.34 = bf16[16,64,512]{2,1,0:T(8,128)(2,1)S(1)} all-to-all(bf16[16,64,512]{2,1,0:T(8,128)(2,1)S(1)} %broadcast_in_dim.27), channel_id=1, replica_groups=mesh['ctx_0'=4,'ctx_1'=4,'tp_0'=4,'tp_1'=2] {'ctx_0','ctx_1'}, dimensions={0} | all-to-all | bytes 2097152 | tf_op jit(solution)/shard_map/all_to_all | solution.py:26
  259.3 1.2 copy.24
  260.4 0.0 all-gather.10.cloned.1.call-update
  260.5 0.2 reduce-window.8
  260.7 51.3 %all-gather.10.cloned.1.call-done = bf16[512,8192]{1,0:T(8,128)(2,1)} async-done(((bf16[64,8192]{1,0:T(8,128)(2,1)}), bf16[512,8192]{1,0:T(8,128)(2,1)}) %all-gather.10.cloned.1.call-update) | async-done | bytes 8388624 | tf_op jit(solution)/shard_map/all_gather | solution.py:229
  312.0 14.2 %fusion.80 = (f32[512]{0:T(512)S(1)}, f32[512,1002]{0,1:T(8,128)S(1)}) fusion(bf16[512,8192]{1,0:T(8,128)(2,1)} %all-gather.10.cloned.1.call-done, bf16[8192,1002]{0,1:T(8,128)(2,1)} %param.21), kind=kOutput, calls=%fused_computation.145 | convolution fusion | flops 8405897728 | bytes 26859520 | tf_op jit(solution)/shard_map/dot_general | solution.py:228
  326.2 0.5 exponential_reduce_fusion
  326.7 9.6 %all-gather.4 = f32[4,3,512]{2,1,0:T(4,128)S(1)} all-gather(f32[1,3,512]{2,1,0:T(4,128)S(1)} %maximum_bitcast_fusion), channel_id=2, replica_groups=mesh['ctx_0'=4,'ctx_1'=4,'tp_0'=4,'tp_1'=2] {'ctx_0'}, dimensions={0}, use_global_device_ids=true | all-gather | bytes 30720 | tf_op jit(solution)/shard_map/all_gather | solution.py:76
  336.4 9.5 %all-gather.5 = f32[4,3,512]{2,1,0:T(4,128)S(1)} all-gather(f32[1,3,512]{2,1,0:T(4,128)S(1)} %maximum_bitcast_fusion.1), channel_id=3, replica_groups=mesh['ctx_0'=4,'ctx_1'=4,'tp_0'=4,'tp_1'=2] {'ctx_1'}, dimensions={0}, use_global_device_ids=true | all-gather | bytes 30720 | tf_op jit(solution)/shard_map/all_gather | solution.py:76
  346.0 9.0 %all-gather.6 = f32[4,3,512]{2,1,0:T(4,128)S(1)} all-gather(f32[1,3,512]{2,1,0:T(4,128)S(1)} %maximum_bitcast_fusion.2), channel_id=4, replica_groups=mesh['ctx_0'=4,'ctx_1'=4,'tp_0'=4,'tp_1'=2] {'tp_0'}, dimensions={0}, use_global_device_ids=true | all-gather | bytes 30720 | tf_op jit(solution)/shard_map/all_gather | solution.py:76
  355.1 10.1 %all-gather.7 = f32[2,3,512]{2,1,0:T(4,128)S(1)} all-gather(f32[1,3,512]{2,1,0:T(4,128)S(1)} %maximum_bitcast_fusion.3), channel_id=5, replica_groups=mesh['ctx_0'=4,'ctx_1'=4,'tp_0'=4,'tp_1'=2] {'tp_1'}, dimensions={0}, use_global_device_ids=true | all-gather | bytes 18432 | tf_op jit(solution)/shard_map/all_gather | solution.py:76
  365.3 0.6 dynamic_slice.10
  365.8 0.7 fusion.20
  (52 shorter events, 0.5 us)
Async XLA Ops:
  7.2 203.5 %copy-start = (bf16[1024,512]{1,0:T(8,128)(2,1)S(1)}, bf16[1024,512]{1,0:T(8,128)(2,1)}, u32[]{:S(2)}) copy-start(bf16[1024,512]{1,0:T(8,128)(2,1)} %param.18) | copy-start | bytes 3145732
  9.3 24.2 %all-to-all-start = ((bf16[16,32,1024]{2,1,0:T(8,128)(2,1)}), bf16[16,32,1024]{2,1,0:T(8,128)(2,1)}, u32[]{:S(2)}, u32[]{:S(2)}) async-start(bf16[16,32,1024]{2,1,0:T(8,128)(2,1)} %broadcast_in_dim.24), calls=%async_computation | async-start | bytes 2097152 | tf_op jit(solution)/shard_map/all_to_all | solution.py:26
  36.1 102.5 %copy-start.3 = (bf16[32,128]{1,0:T(8,128)(2,1)S(1)}, bf16[32,128]{1,0:T(8,128)(2,1)}, u32[]{:S(2)}) copy-start(bf16[32,128]{1,0:T(8,128)(2,1)} %param.16) | copy-start | bytes 24580
  138.7 1.9 copy-start.4
  187.7 1.0 copy-start.1
  210.6 10.7 %copy-start.6 = (bf16[512]{0:T(512)(128)(2,1)S(1)}, bf16[512]{0:T(512)(128)(2,1)}, u32[]{:S(2)}) copy-start(bf16[512]{0:T(512)(128)(2,1)} %param.20) | copy-start | bytes 3076
  210.6 20.1 %copy-start.2 = (bf16[64,512]{1,0:T(8,128)(2,1)S(1)}, bf16[64,512]{1,0:T(8,128)(2,1)}, u32[]{:S(2)}) copy-start(bf16[64,512]{1,0:T(8,128)(2,1)} %param.19) | copy-start | bytes 196612
  212.1 18.5 %all-to-all-start.3 = ((bf16[8,64,512]{2,1,0:T(8,128)(2,1)}), bf16[8,64,512]{2,1,0:T(8,128)(2,1)S(1)}, u32[]{:S(2)}, u32[]{:S(2)}) async-start(bf16[8,64,512]{2,1,0:T(8,128)(2,1)} %bitcast.12), calls=%async_computation.3 | async-start | bytes 1048576 | tf_op jit(solution)/shard_map/all_to_all | solution.py:58
  221.3 90.7 %all-gather.10.cloned.1.call-start = ((), (), s32[]{:S(2)}) async-start(), calls=%async_computation.5 | async-start | bytes 9437184 | tf_op jit(solution)/shard_map/all_gather | solution.py:229
  259.3 1.2 copy-start.7
  260.7 65.5 %copy-start.5 = (s32[512]{0:T(512)S(1)}, s32[512]{0:T(512)}, u32[]{:S(2)}) copy-start(s32[512]{0:T(512)} %param.22) | copy-start | bytes 6148
Sparse Core Ops, SparseCore 0:
  260.6 51.3 all-gather.9
where the time goes:
time: 374 us; the launch traced here: 373 us
  blocking collectives  102 us (27%)
  matrix products  88.1 us (24%)
  waiting for transfers between devices  76.3 us (20%)
  other arithmetic  47.7 us (13%)
  local copies, waits for them, and re-layouts  27.5 us (7%)
  starting transfers between devices  17.6 us (5%)
  between operations  14.4 us (4%)
    all_gather x1, waiting for transfers between devices, local(): lax.all_gather(normed_rows, TP, axis=0, tiled=True)  51.3 us
    all_gather x4, blocking collectives, gathered_once(): both, at, found = (lax.all_gather(jnp.concatenate(lines), axis), 0, {})  38.3 us
    dot_general x4, matrix products, advance(): jnp.dot(query_rows, block_pair[0].T, preferred_element_type=jnp.float32)  37.5 us
    reduce_sum x5, other arithmetic, fold_block(): row_sum = row_sum * fading + jnp.sum(weights, axis=1)  34.2 us
    dot_general x5, matrix products, fold_block(): jnp.dot(weights.astype(jnp.bfloat16), value_rows, preferred_element_type=...  32.5 us
    all_to_all x2, blocking collectives, sent_to_all(): lax.all_to_all(jnp.broadcast_to(value[None], (count, *value.shape)), axis...  31.2 us
    all_to_all x1, blocking collectives, sent_together(): lax.all_to_all(both, axis, split_axis=split_dim, concat_axis=concat_dim,...  18.9 us
    all_to_all x1, waiting for transfers between devices, sent_to_all(): lax.all_to_all(jnp.broadcast_to(value[None], (count, *value.shape)), axis...  15.7 us
  transfers between devices with their start and end apart: 3, of which 3 were waited for; matrix products, arithmetic and copies ran while one was open for 0% of the time, Pallas kernels for 0%

commit v1 on v0

--- a/solution.py
+++ b/solution.py
@@ -226,7 +226,9 @@
     )
     normed_rows = gathered_copies(normed_part, CTX, 1)
     logits = jnp.dot(
-        lax.all_gather(normed_rows, TP, axis=0, tiled=True),
+        jnp.concatenate(
+            lax.all_to_all(jnp.stack([normed_rows] * lax.axis_size(TP)), TP, 0, 0), axis=0
+        ),
         head_weight,
         preferred_element_type=jnp.float32,
     )

time: 374 us -> 417 us (1.11)
  waiting for transfers between devices: 76.3 us -> 119 us
  between operations: 14.4 us -> 1 us
  starting transfers between devices: 17.6 us -> 28.6 us
    all_to_all x0 -> x1, waiting for transfers between devices: none -> 93.6 us  [local(): lax.all_to_all(jnp.stack([normed_rows] * lax.axis_size(TP)), TP, 0, 0)]
    all_gather x1 -> x0, waiting for transfers between devices: 51.3 us -> none  [local(): lax.all_gather(normed_rows, TP, axis=0, tiled=True)]
    all_to_all x0 -> x1, starting transfers between devices: none -> 11 us  [local(): lax.all_to_all(jnp.stack([normed_rows] * lax.axis_size(TP)), TP, 0, 0)]
    another operation x0 -> x2, local copies, waits for them, and re-layouts: none -> 4.32 us  [local(): jnp.stack([normed_rows] * lax.axis_size(TP))]
where the time goes in v1:
time: 417 us; the launch traced here: 416 us
  waiting for transfers between devices  119 us (29%)
  blocking collectives  101 us (24%)
  matrix products  88.1 us (21%)
  other arithmetic  47.7 us (11%)
  local copies, waits for them, and re-layouts  30.7 us (7%)
  starting transfers between devices  28.6 us (7%)
    all_to_all x1, waiting for transfers between devices, local(): lax.all_to_all(jnp.stack([normed_rows] * lax.axis_size(TP)), TP, 0, 0)  93.6 us
    all_gather x4, blocking collectives, gathered_once(): both, at, found = (lax.all_gather(jnp.concatenate(lines), axis), 0, {})  38.2 us
    dot_general x4, matrix products, advance(): jnp.dot(query_rows, block_pair[0].T, preferred_element_type=jnp.float32)  37.5 us
    reduce_sum x5, other arithmetic, fold_block(): row_sum = row_sum * fading + jnp.sum(weights, axis=1)  34.2 us
    dot_general x5, matrix products, fold_block(): jnp.dot(weights.astype(jnp.bfloat16), value_rows, preferred_element_type=...  32.5 us
    all_to_all x2, blocking collectives, sent_to_all(): lax.all_to_all(jnp.broadcast_to(value[None], (count, *value.shape)), axis...  31.2 us
    all_to_all x1, blocking collectives, sent_together(): lax.all_to_all(both, axis, split_axis=split_dim, concat_axis=concat_dim,...  18.9 us
    all_to_all x1, waiting for transfers between devices, sent_to_all(): lax.all_to_all(jnp.broadcast_to(value[None], (count, *value.shape)), axis...  15.7 us
  transfers between devices with their start and end apart: 3, of which 3 were waited for; matrix products, arithmetic and copies ran while one was open for 0% of the time, Pallas kernels for 0%

profile of v1, /device:TPU:1, one launch (start us, length us, event | category | flops | bytes accessed | tf_op | source)
XLA Modules:
  0.0 416.3 jit_solution(2352424080007007937)
XLA Ops:
  0.6 0.0 copy-start
  0.6 2.1 broadcast_in_dim.24
  2.7 8.5 %all-to-all-start = ((bf16[16,32,1024]{2,1,0:T(8,128)(2,1)}), bf16[16,32,1024]{2,1,0:T(8,128)(2,1)}, u32[]{:S(2)}, u32[]{:S(2)}) async-start(bf16[16,32,1024]{2,1,0:T(8,128)(2,1)} %broadcast_in_dim.24), calls=%async_computation | async-start | bytes 2097152 | tf_op jit(solution)/shard_map/all_to_all | solution.py:26
  11.3 15.7 %all-to-all-done = bf16[16,32,1024]{2,1,0:T(8,128)(2,1)} async-done(((bf16[16,32,1024]{2,1,0:T(8,128)(2,1)}), bf16[16,32,1024]{2,1,0:T(8,128)(2,1)}, u32[]{:S(2)}, u32[]{:S(2)}) %all-to-all-start) | async-done | bytes 1048608 | tf_op jit(solution)/shard_map/all_to_all | solution.py:26
  26.9 1.5 copy.25
  28.4 1.2 copy.19
  29.6 102.5 %while.15 = (s32[]{:T(128)}, f32[4096]{0:T(1024)S(1)}, f32[4096]{0:T(1024)S(1)}, f32[4096,128]{1,0:T(8,128)S(1)}, bf16[4,1024,128]{2,1,0:T(8,128)(2,1)}, /*index...) while((s32[]{:T(128)}, f32[4096]{0:T(1024)S(1)}, ...), condition=%wide.region_3.4_spmd.clone, body=%wide.region_0.3_spmd.clone.sunk | while | flops 2182631424 | bytes 56361076 | solution.py:125
  29.6 9.4 %multiply_reduce_fusion.5 = (f32[4096]{0:T(1024)S(1)}, f32[1024,4096]{1,0:T(8,128)}) fusion(bf16[4096,128]{1,0:T(8,128)(2,1)} %get-tuple-element.183, bf16[4,1024,128]{2,1,0:T(8,128)(2,1)} %get-tuple-element.182, s32[]{:T(128)S(6)} %copy.32), kind=kOutput, calls=%fused_computation.1.clone.1 | convolution fusion | flops 1082126336 | bytes 18104324 | tf_op jit(solution)/shard_map/while/body/eval_jaxpr/dot_general | solution.py:117
  39.0 8.5 %fusion.99 = f32[4096]{0:T(1024)S(1)} fusion(f32[1024,4096]{1,0:T(8,128)} %get-tuple-element.157, f32[4096]{0:T(1024)S(1)} %select_maximum_fusion.2), kind=kLoop, calls=%fused_computation.3.clone.1 | loop fusion | flops 12578816 | bytes 16809984 | tf_op jit(solution)/shard_map/while/body/eval_jaxpr/reduce_sum | solution.py:99
  47.5 7.7 %fusion.101 = f32[4096,128]{1,0:T(8,128)S(1)} fusion(f32[1024,4096]{1,0:T(8,128)} %get-tuple-element.157, f32[4096]{0:T(1024)S(1)} %select_maximum_fusion.2, f32[4096,128]{1,0:T(8,128)S(1)} %get-tuple-element.172, f32[4096]{0:T(1024)S(1)} %get-tuple-element.159, pred[]{:T(512)S(6)} %compare.4, bf16[4,1024,128]{2,1,0:T(8,128)(2,1)} %get-tuple-element.184, ...), kind=kOutput, calls=%fused_computation.7.clone.1 | convolution fusion | flops 1087897600 | bytes 21266436 | tf_op jit(solution)/shard_map/while/body/eval_jaxpr/dot_general | solution.py:100
  55.2 9.4 %multiply_reduce_fusion.5 = (f32[4096]{0:T(1024)S(1)}, f32[1024,4096]{1,0:T(8,128)}) fusion(bf16[4096,128]{1,0:T(8,128)(2,1)} %get-tuple-element.183, bf16[4,1024,128]{2,1,0:T(8,128)(2,1)} %get-tuple-element.182, s32[]{:T(128)S(6)} %copy.32), kind=kOutput, calls=%fused_computation.1.clone.1 | convolution fusion | flops 1082126336 | bytes 18104324 | tf_op jit(solution)/shard_map/while/body/eval_jaxpr/dot_general | solution.py:117
  64.6 8.5 %fusion.99 = f32[4096]{0:T(1024)S(1)} fusion(f32[1024,4096]{1,0:T(8,128)} %get-tuple-element.157, f32[4096]{0:T(1024)S(1)} %select_maximum_fusion.2), kind=kLoop, calls=%fused_computation.3.clone.1 | loop fusion | flops 12578816 | bytes 16809984 | tf_op jit(solution)/shard_map/while/body/eval_jaxpr/reduce_sum | solution.py:99
  73.2 7.7 %fusion.101 = f32[4096,128]{1,0:T(8,128)S(1)} fusion(f32[1024,4096]{1,0:T(8,128)} %get-tuple-element.157, f32[4096]{0:T(1024)S(1)} %select_maximum_fusion.2, f32[4096,128]{1,0:T(8,128)S(1)} %get-tuple-element.172, f32[4096]{0:T(1024)S(1)} %get-tuple-element.159, pred[]{:T(512)S(6)} %compare.4, bf16[4,1024,128]{2,1,0:T(8,128)(2,1)} %get-tuple-element.184, ...), kind=kOutput, calls=%fused_computation.7.clone.1 | convolution fusion | flops 1087897600 | bytes 21266436 | tf_op jit(solution)/shard_map/while/body/eval_jaxpr/dot_general | solution.py:100
  80.9 9.4 %multiply_reduce_fusion.5 = (f32[4096]{0:T(1024)S(1)}, f32[1024,4096]{1,0:T(8,128)}) fusion(bf16[4096,128]{1,0:T(8,128)(2,1)} %get-tuple-element.183, bf16[4,1024,128]{2,1,0:T(8,128)(2,1)} %get-tuple-element.182, s32[]{:T(128)S(6)} %copy.32), kind=kOutput, calls=%fused_computation.1.clone.1 | convolution fusion | flops 1082126336 | bytes 18104324 | tf_op jit(solution)/shard_map/while/body/eval_jaxpr/dot_general | solution.py:117
  90.2 8.5 %fusion.99 = f32[4096]{0:T(1024)S(1)} fusion(f32[1024,4096]{1,0:T(8,128)} %get-tuple-element.157, f32[4096]{0:T(1024)S(1)} %select_maximum_fusion.2), kind=kLoop, calls=%fused_computation.3.clone.1 | loop fusion | flops 12578816 | bytes 16809984 | tf_op jit(solution)/shard_map/while/body/eval_jaxpr/reduce_sum | solution.py:99
  98.8 7.7 %fusion.101 = f32[4096,128]{1,0:T(8,128)S(1)} fusion(f32[1024,4096]{1,0:T(8,128)} %get-tuple-element.157, f32[4096]{0:T(1024)S(1)} %select_maximum_fusion.2, f32[4096,128]{1,0:T(8,128)S(1)} %get-tuple-element.172, f32[4096]{0:T(1024)S(1)} %get-tuple-element.159, pred[]{:T(512)S(6)} %compare.4, bf16[4,1024,128]{2,1,0:T(8,128)(2,1)} %get-tuple-element.184, ...), kind=kOutput, calls=%fused_computation.7.clone.1 | convolution fusion | flops 1087897600 | bytes 21266436 | tf_op jit(solution)/shard_map/while/body/eval_jaxpr/dot_general | solution.py:100
  106.5 9.4 %multiply_reduce_fusion.5 = (f32[4096]{0:T(1024)S(1)}, f32[1024,4096]{1,0:T(8,128)}) fusion(bf16[4096,128]{1,0:T(8,128)(2,1)} %get-tuple-element.183, bf16[4,1024,128]{2,1,0:T(8,128)(2,1)} %get-tuple-element.182, s32[]{:T(128)S(6)} %copy.32), kind=kOutput, calls=%fused_computation.1.clone.1 | convolution fusion | flops 1082126336 | bytes 18104324 | tf_op jit(solution)/shard_map/while/body/eval_jaxpr/dot_general | solution.py:117
  115.9 8.5 %fusion.99 = f32[4096]{0:T(1024)S(1)} fusion(f32[1024,4096]{1,0:T(8,128)} %get-tuple-element.157, f32[4096]{0:T(1024)S(1)} %select_maximum_fusion.2), kind=kLoop, calls=%fused_computation.3.clone.1 | loop fusion | flops 12578816 | bytes 16809984 | tf_op jit(solution)/shard_map/while/body/eval_jaxpr/reduce_sum | solution.py:99
  124.4 7.7 %fusion.101 = f32[4096,128]{1,0:T(8,128)S(1)} fusion(f32[1024,4096]{1,0:T(8,128)} %get-tuple-element.157, f32[4096]{0:T(1024)S(1)} %select_maximum_fusion.2, f32[4096,128]{1,0:T(8,128)S(1)} %get-tuple-element.172, f32[4096]{0:T(1024)S(1)} %get-tuple-element.159, pred[]{:T(512)S(6)} %compare.4, bf16[4,1024,128]{2,1,0:T(8,128)(2,1)} %get-tuple-element.184, ...), kind=kOutput, calls=%fused_computation.7.clone.1 | convolution fusion | flops 1087897600 | bytes 21266436 | tf_op jit(solution)/shard_map/while/body/eval_jaxpr/dot_general | solution.py:100
  132.1 0.0 copy-start.4
  132.1 1.7 fusion.79
  133.9 0.1 fusion.22
  134.0 0.0 copy-done.4
  134.0 1.8 fusion.18
  135.8 1.5 copy.20
  137.4 1.1 pad_maximum_fusion
  138.4 5.2 %copy.21 = bf16[1,512,1040]{2,0,1:T(2,128)(2,1)S(1)} copy(bf16[1,512,1040]{1,2,0:T(8,128)(2,1)} %pad_maximum_fusion) | data formatting | bytes 2129920 | tf_op jit(solution)/shard_map/concatenate | solution.py:40
  143.7 0.5 broadcast.83
  144.2 9.2 %reduce.4 = bf16[512,1040]{1,0:T(8,128)(2,1)} reduce(bf16[512,1,1040]{2,1,0:T(2,128)(2,1)S(1)} %bitcast.307, bf16[]{:T(256)} %broadcast.83), dimensions={1}, to_apply=%bitcast.274.reduce_sub_computation | reduce | bytes 2129922
  153.4 3.9 reshape.903
  157.3 18.9 %all_to_all.37 = bf16[16,2,16640]{2,1,0:T(2,128)(2,1)} all-to-all(bf16[16,2,16640]{2,1,0:T(2,128)(2,1)S(1)} %reshape.903), channel_id=1, replica_groups=mesh['ctx_0'=4,'ctx_1'=4,'tp_0'=4,'tp_1'=2] {'ctx_0','ctx_1'}, dimensions={0} | all-to-all | bytes 2129920 | tf_op jit(solution)/shard_map/all_to_all | solution.py:43
  176.2 4.8 %reshape.904 = bf16[512,1,1040]{2,1,0:T(2,128)(2,1)S(1)} reshape(bf16[16,2,16640]{2,1,0:T(2,128)(2,1)} %all_to_all.37) | data formatting | bytes 2129920
  181.0 0.2 copy.23
  181.2 0.1 multiply_reduce_fusion.2
  181.4 0.9 copy-done.1
  182.2 2.0 mul.276
  184.2 1.7 mul.277
  185.9 1.8 multiply_reduce_fusion.1
  187.7 0.1 div.24
  187.8 0.1 broadcast_in_dim.26
  188.0 16.1 %all_to_all.38 = bf16[16,32,1024]{2,1,0:T(8,128)(2,1)S(1)} all-to-all(bf16[16,32,1024]{2,1,0:T(8,128)(2,1)S(1)} %broadcast_in_dim.26), channel_id=1, replica_groups=mesh['ctx_0'=4,'ctx_1'=4,'tp_0'=4,'tp_1'=2] {'ctx_0','ctx_1'}, dimensions={0} | all-to-all | bytes 2097152 | tf_op jit(solution)/shard_map/all_to_all | solution.py:26
  204.1 1.5 convolution_convert_fusion
  205.6 9.2 %all-to-all-start.3 = ((bf16[8,64,512]{2,1,0:T(8,128)(2,1)}), bf16[8,64,512]{2,1,0:T(8,128)(2,1)S(1)}, u32[]{:S(2)}, u32[]{:S(2)}) async-start(bf16[8,64,512]{2,1,0:T(8,128)(2,1)} %bitcast.12), calls=%async_computation.3 | async-start | bytes 1048576 | tf_op jit(solution)/shard_map/all_to_all | solution.py:58
  214.8 9.3 %all-to-all-done.3 = bf16[8,64,512]{2,1,0:T(8,128)(2,1)S(1)} async-done(((bf16[8,64,512]{2,1,0:T(8,128)(2,1)}), bf16[8,64,512]{2,1,0:T(8,128)(2,1)S(1)}, u32[]{:S(2)}, u32[]{:S(2)}) %all-to-all-start.3) | async-done | bytes 524320 | tf_op jit(solution)/shard_map/all_to_all | solution.py:58
  224.1 0.1 convert_reduce_fusion
  224.2 0.1 multiply_reduce_fusion.3
  224.3 6.8 %psum.14 = f32[64]{0:T(128)S(1)} all-reduce(f32[64]{0:T(128)S(1)} %multiply_reduce_fusion.3), channel_id=1, replica_groups=mesh['ctx_0'=4,'ctx_1'=4,'tp_0'=4,'tp_1'=2] {'ctx_0'}, use_global_device_ids=true, to_apply=%region_11.12 | all-reduce | flops 64 | bytes 512 | tf_op jit(solution)/shard_map/psum | solution.py:64
  231.1 6.3 %psum.15 = f32[64]{0:T(128)S(1)} all-reduce(f32[64]{0:T(128)S(1)} %psum.14), channel_id=1, replica_groups=mesh['ctx_0'=4,'ctx_1'=4,'tp_0'=4,'tp_1'=2] {'ctx_1'}, use_global_device_ids=true, to_apply=%region_12.13 | all-reduce | flops 64 | bytes 512 | tf_op jit(solution)/shard_map/psum | solution.py:64
  237.5 0.1 multiply_convert_fusion
  237.6 0.1 broadcast_in_dim.27
  237.7 15.1 %all_to_all.39 = bf16[16,64,512]{2,1,0:T(8,128)(2,1)S(1)} all-to-all(bf16[16,64,512]{2,1,0:T(8,128)(2,1)S(1)} %broadcast_in_dim.27), channel_id=1, replica_groups=mesh['ctx_0'=4,'ctx_1'=4,'tp_0'=4,'tp_1'=2] {'ctx_0','ctx_1'}, dimensions={0} | all-to-all | bytes 2097152 | tf_op jit(solution)/shard_map/all_to_all | solution.py:26
  252.7 0.1 copy.24
  252.8 4.2 %stack.3 = bf16[8,64,8192]{2,1,0:T(8,128)(2,1)} broadcast(bf16[64,8192]{1,0:T(8,128)(2,1)S(1)} %bitcast.312), dimensions={1,2} | broadcast | bytes 9437184 | tf_op jit(solution)/shard_map/stack | solution.py:230
  257.1 11.0 %all-to-all-start.5 = ((bf16[8,64,8192]{2,1,0:T(8,128)(2,1)}), bf16[8,64,8192]{2,1,0:T(8,128)(2,1)}, u32[]{:S(2)}, u32[]{:S(2)}) async-start(bf16[8,64,8192]{2,1,0:T(8,128)(2,1)} %stack.3), calls=%async_computation.5 | async-start | bytes 16777216 | tf_op jit(solution)/shard_map/all_to_all | solution.py:230
  268.1 0.2 reduce-window.8
  268.3 93.6 %all-to-all-done.5 = bf16[8,64,8192]{2,1,0:T(8,128)(2,1)} async-done(((bf16[8,64,8192]{2,1,0:T(8,128)(2,1)}), bf16[8,64,8192]{2,1,0:T(8,128)(2,1)}, u32[]{:S(2)}, u32[]{:S(2)}) %all-to-all-start.5) | async-done | bytes 8388640 | tf_op jit(solution)/shard_map/all_to_all | solution.py:230
  361.8 14.2 %fusion.80 = (f32[512]{0:T(512)S(1)}, f32[512,1002]{0,1:T(8,128)S(1)}) fusion(bf16[512,8192]{1,0:T(8,128)(2,1)} %bitcast.14, bf16[8192,1002]{0,1:T(8,128)(2,1)} %param.21), kind=kOutput, calls=%fused_computation.145 | convolution fusion | flops 8405897728 | bytes 26859520 | tf_op jit(solution)/shard_map/dot_general | solution.py:228
  376.1 0.5 exponential_reduce_fusion
  376.6 9.0 %all-gather.4 = f32[4,3,512]{2,1,0:T(4,128)S(1)} all-gather(f32[1,3,512]{2,1,0:T(4,128)S(1)} %maximum_bitcast_fusion), channel_id=2, replica_groups=mesh['ctx_0'=4,'ctx_1'=4,'tp_0'=4,'tp_1'=2] {'ctx_0'}, dimensions={0}, use_global_device_ids=true | all-gather | bytes 30720 | tf_op jit(solution)/shard_map/all_gather | solution.py:76
  385.7 9.0 %all-gather.5 = f32[4,3,512]{2,1,0:T(4,128)S(1)} all-gather(f32[1,3,512]{2,1,0:T(4,128)S(1)} %maximum_bitcast_fusion.1), channel_id=3, replica_groups=mesh['ctx_0'=4,'ctx_1'=4,'tp_0'=4,'tp_1'=2] {'ctx_1'}, dimensions={0}, use_global_device_ids=true | all-gather | bytes 30720 | tf_op jit(solution)/shard_map/all_gather | solution.py:76
  394.8 9.0 %all-gather.6 = f32[4,3,512]{2,1,0:T(4,128)S(1)} all-gather(f32[1,3,512]{2,1,0:T(4,128)S(1)} %maximum_bitcast_fusion.2), channel_id=4, replica_groups=mesh['ctx_0'=4,'ctx_1'=4,'tp_0'=4,'tp_1'=2] {'tp_0'}, dimensions={0}, use_global_device_ids=true | all-gather | bytes 30720 | tf_op jit(solution)/shard_map/all_gather | solution.py:76
  403.9 11.1 %all-gather.7 = f32[2,3,512]{2,1,0:T(4,128)S(1)} all-gather(f32[1,3,512]{2,1,0:T(4,128)S(1)} %maximum_bitcast_fusion.3), channel_id=5, replica_groups=mesh['ctx_0'=4,'ctx_1'=4,'tp_0'=4,'tp_1'=2] {'tp_1'}, dimensions={0}, use_global_device_ids=true | all-gather | bytes 18432 | tf_op jit(solution)/shard_map/all_gather | solution.py:76
  415.0 0.6 dynamic_slice.10
  415.6 0.7 fusion.20
  (52 shorter events, 0.5 us)
Async XLA Ops:
  0.6 203.5 %copy-start = (bf16[1024,512]{1,0:T(8,128)(2,1)S(1)}, bf16[1024,512]{1,0:T(8,128)(2,1)}, u32[]{:S(2)}) copy-start(bf16[1024,512]{1,0:T(8,128)(2,1)} %param.18) | copy-start | bytes 3145732
  2.7 24.2 %all-to-all-start = ((bf16[16,32,1024]{2,1,0:T(8,128)(2,1)}), bf16[16,32,1024]{2,1,0:T(8,128)(2,1)}, u32[]{:S(2)}, u32[]{:S(2)}) async-start(bf16[16,32,1024]{2,1,0:T(8,128)(2,1)} %broadcast_in_dim.24), calls=%async_computation | async-start | bytes 2097152 | tf_op jit(solution)/shard_map/all_to_all | solution.py:26
  29.6 102.5 %copy-start.3 = (bf16[32,128]{1,0:T(8,128)(2,1)S(1)}, bf16[32,128]{1,0:T(8,128)(2,1)}, u32[]{:S(2)}) copy-start(bf16[32,128]{1,0:T(8,128)(2,1)} %param.16) | copy-start | bytes 24580
  132.1 1.9 copy-start.4
  181.2 1.0 copy-start.1
  204.1 10.7 %copy-start.6 = (bf16[512]{0:T(512)(128)(2,1)S(1)}, bf16[512]{0:T(512)(128)(2,1)}, u32[]{:S(2)}) copy-start(bf16[512]{0:T(512)(128)(2,1)} %param.20) | copy-start | bytes 3076
  204.1 20.1 %copy-start.2 = (bf16[64,512]{1,0:T(8,128)(2,1)S(1)}, bf16[64,512]{1,0:T(8,128)(2,1)}, u32[]{:S(2)}) copy-start(bf16[64,512]{1,0:T(8,128)(2,1)} %param.19) | copy-start | bytes 196612
  205.6 18.5 %all-to-all-start.3 = ((bf16[8,64,512]{2,1,0:T(8,128)(2,1)}), bf16[8,64,512]{2,1,0:T(8,128)(2,1)S(1)}, u32[]{:S(2)}, u32[]{:S(2)}) async-start(bf16[8,64,512]{2,1,0:T(8,128)(2,1)} %bitcast.12), calls=%async_computation.3 | async-start | bytes 1048576 | tf_op jit(solution)/shard_map/all_to_all | solution.py:58
  257.1 11.0 %copy-start.7 = (s32[8]{0:T(128)S(1)}, s32[8]{0:T(128)}, u32[]{:S(2)}) copy-start(s32[8]{0:T(128)} %param.23) | copy-start | bytes 100
  257.1 104.8 %all-to-all-start.5 = ((bf16[8,64,8192]{2,1,0:T(8,128)(2,1)}), bf16[8,64,8192]{2,1,0:T(8,128)(2,1)}, u32[]{:S(2)}, u32[]{:S(2)}) async-start(bf16[8,64,8192]{2,1,0:T(8,128)(2,1)} %stack.3), calls=%async_computation.5 | async-start | bytes 16777216 | tf_op jit(solution)/shard_map/all_to_all | solution.py:230
  361.8 14.2 %copy-start.5 = (s32[512]{0:T(512)S(1)}, s32[512]{0:T(512)}, u32[]{:S(2)}) copy-start(s32[512]{0:T(512)} %param.22) | copy-start | bytes 6148
